TPU v7x, 32 devices: a 4x4x1 block of a 4x4x8 slice. The times are simulated.
32 devices in a mesh: rep: 1 (over z), kv: 32 (over y, x, core).
Axes of the slice: x: 4, y: 4, z: 1, core: 2. Of those that a mesh axis runs over, the one named last changes fastest.
The devices are a block of a 4x4x8 slice.
Arguments:
- embeds: bfloat16 [2, 128, 2048], P(None, ('rep', 'kv'))
- w_query: bfloat16 [2, 2048, 2048], replicated
- w_key: bfloat16 [2, 2048, 2048], replicated
- w_value: bfloat16 [2, 2048, 2048], replicated
- w_out: bfloat16 [2, 2048, 2048], replicated
- w_up: bfloat16 [2, 2048, 8192], replicated
- w_down: bfloat16 [2, 8192, 2048], replicated
- k_pool: bfloat16 [2304, 2, 16, 16, 128], P(('rep', 'kv'))
- v_pool: bfloat16 [2304, 2, 16, 16, 128], P(('rep', 'kv'))
- old_table: int32 [128, 12], P('rep')
- new_table: int32 [128, 12], P('rep')
- seq_len: int32 [128], P('rep')
- finished: int32 [128], P('rep')
- mig_src: int32 [768], P('rep')
- mig_dst: int32 [768], P('rep')
Outputs:
- output 1: bfloat16 [2, 128, 2048], P(None, ('rep', 'kv'))
- output 2: bfloat16 [2304, 2, 16, 16, 128], P(('rep', 'kv'))
- output 3: bfloat16 [2304, 2, 16, 16, 128], P(('rep', 'kv'))
All inputs are finite; a program needn't handle non-finite values.
Results may differ from a plain program's by a relative error of at most 0.0188525.
Values are sent between devices in bfloat16 or wider.
A program may use at most 768 MiB of HBM per device.

v0:
```python
import jax
import jax.numpy as jnp
from jax import lax
from jax.sharding import PartitionSpec as P


def solution(mesh):
    groups = mesh.shape['kv']
    rows_spec = P(None, ('rep', 'kv'), None)
    pool_spec = P(('rep', 'kv'))
    table_spec = P('rep', None)
    vec_spec = P('rep')
    full_spec = P()

    def device_fn(embeds, w_query, w_key, w_value, w_out, w_up, w_down, k_pool, v_pool, old_table, new_table, seq_len, finished, mig_src, mig_dst):
        my_dev = lax.axis_index('kv')
        slots_dev, n_layers, page_size, kv_heads, head_dim = k_pool.shape
        seq_dev = embeds.shape[1]
        n_batch, pages_seq = old_table.shape
        q_width = w_query.shape[2]
        kv_width = kv_heads * head_dim
        rep_factor = q_width // kv_width
        n_mig = mig_src.shape[0]
        pair_cap = 4 * n_mig // (groups * groups)
        score_scale = head_dim ** -0.5
        slot_base = my_dev * slots_dev
        seq_ids = jnp.arange(n_batch, dtype=jnp.int32)
        active = finished == 0
        len_next = seq_len + 1
        home_done = lax.dynamic_slice(finished, (my_dev * seq_dev,), (seq_dev,))

        def slot_maps(table, only_active):
            local_slot = table - slot_base
            keep_mask = (local_slot >= 0) & (local_slot < slots_dev)
            if only_active:
                keep_mask = keep_mask & active[:, None]
            target = jnp.where(keep_mask, local_slot, slots_dev).reshape(-1)
            slot_owner = jnp.full((slots_dev,), n_batch, jnp.int32).at[target].set(jnp.repeat(seq_ids, pages_seq), mode='drop')
            slot_page = jnp.zeros((slots_dev,), jnp.int32).at[target].set(jnp.tile(jnp.arange(pages_seq, dtype=jnp.int32), n_batch), mode='drop')
            return slot_owner, slot_page

        def project_all(hidden, layer_idx):
            query_loc = jnp.dot(hidden, w_query[layer_idx], preferred_element_type=jnp.float32).astype(jnp.bfloat16)
            k_loc = jnp.dot(hidden, w_key[layer_idx], preferred_element_type=jnp.float32).astype(jnp.bfloat16)
            v_loc = jnp.dot(hidden, w_value[layer_idx], preferred_element_type=jnp.float32).astype(jnp.bfloat16)
            packed = jnp.concatenate([query_loc, k_loc, v_loc], axis=1)
            gathered = lax.all_gather(packed, 'kv', axis=0, tiled=True)
            query_rows = gathered[:, :q_width]
            k_new = gathered[:, q_width:q_width + kv_width].reshape(n_batch, kv_heads, head_dim)
            v_new = gathered[:, q_width + kv_width:].reshape(n_batch, kv_heads, head_dim)
            return query_rows, k_new, v_new

        def write_new(k_layer, v_layer, k_new, v_new, table, lengths, only_active):
            page_now = lengths // page_size
            local_slot = jnp.take_along_axis(table, page_now[:, None], axis=1)[:, 0] - slot_base
            keep_mask = (local_slot >= 0) & (local_slot < slots_dev)
            if only_active:
                keep_mask = keep_mask & active
            write_rows = jnp.where(keep_mask, local_slot, slots_dev)
            offset = lengths % page_size
            return k_layer.at[write_rows, offset].set(k_new, mode='drop'), v_layer.at[write_rows, offset].set(v_new, mode='drop')

        def to_home(values):
            return lax.all_to_all(values, 'kv', 0, 0, tiled=True)

        def attend(query_rows, k_layer, v_layer, slot_owner, slot_page, lengths):
            q_slot = jnp.take(query_rows, slot_owner, axis=0, mode='clip').reshape(slots_dev, kv_heads, rep_factor, head_dim)
            scores = jnp.einsum('sgrd,spgd->sgrp', q_slot, k_layer, preferred_element_type=jnp.float32) * score_scale
            len_slot = jnp.take(lengths, slot_owner, mode='clip')
            positions = slot_page[:, None] * page_size + jnp.arange(page_size)[None, :]
            valid_pos = (positions <= len_slot[:, None]) & (slot_owner < n_batch)[:, None]
            scores = jnp.where(valid_pos[:, None, None, :], scores, -1e30)
            slot_max = scores.max(axis=-1)
            exp_scores = jnp.exp(scores - slot_max[..., None])
            slot_sum = exp_scores.sum(axis=-1)
            slot_out = jnp.einsum('sgrp,spgd->sgrd', exp_scores.astype(jnp.bfloat16), v_layer, preferred_element_type=jnp.float32)
            seq_max = jnp.full((n_batch, kv_heads, rep_factor), -jnp.inf, jnp.float32).at[slot_owner].max(slot_max, mode='drop')
            factor = jnp.exp(slot_max - jnp.take(seq_max, slot_owner, axis=0, mode='clip'))
            seq_sum = jax.ops.segment_sum(slot_sum * factor, slot_owner, num_segments=n_batch)
            seq_out = jax.ops.segment_sum(slot_out * factor[..., None], slot_owner, num_segments=n_batch)
            stats_home = to_home(jnp.stack([seq_max, seq_sum], axis=1)).reshape(groups, seq_dev, 2, kv_heads, rep_factor)
            out_home = to_home(seq_out).reshape(groups, seq_dev, kv_heads, rep_factor, head_dim)
            top_max = stats_home[:, :, 0].max(axis=0)
            top_max = jnp.where(jnp.isfinite(top_max), top_max, 0.0)
            weight_home = jnp.exp(stats_home[:, :, 0] - top_max)
            total_sum = (stats_home[:, :, 1] * weight_home).sum(axis=0)
            acc_home = (out_home * weight_home[..., None]).sum(axis=0)
            result = acc_home / jnp.where(total_sum > 0, total_sum, 1.0)[..., None]
            return result.astype(jnp.bfloat16).reshape(seq_dev, q_width)

        def finish_block(hidden, attn_rows, layer_idx):
            mixed_rows = (hidden.astype(jnp.float32) + jnp.dot(attn_rows, w_out[layer_idx], preferred_element_type=jnp.float32)).astype(jnp.bfloat16)
            inner_act = jax.nn.gelu(jnp.dot(mixed_rows, w_up[layer_idx], preferred_element_type=jnp.float32)).astype(jnp.bfloat16)
            return (mixed_rows.astype(jnp.float32) + jnp.dot(inner_act, w_down[layer_idx], preferred_element_type=jnp.float32)).astype(jnp.bfloat16)

        src_dev = mig_src // slots_dev
        dst_dev = mig_dst // slots_dev
        pair_key = src_dev * groups + dst_dev
        order_idx = jnp.argsort(pair_key, stable=True)
        sorted_key = pair_key[order_idx]
        first_pos = jnp.searchsorted(sorted_key, sorted_key, side='left')
        pair_rank = jnp.zeros((n_mig,), jnp.int32).at[order_idx].set(jnp.arange(n_mig, dtype=jnp.int32) - first_pos)
        send_pos = jnp.where(src_dev == my_dev, dst_dev * pair_cap + pair_rank, groups * pair_cap)
        send_slot = jnp.zeros((groups * pair_cap,), jnp.int32).at[send_pos].set(mig_src - slot_base, mode='drop')
        recv_pos = jnp.where(dst_dev == my_dev, src_dev * pair_cap + pair_rank, groups * pair_cap)
        recv_slot = jnp.full((groups * pair_cap,), slots_dev, jnp.int32).at[recv_pos].set(mig_dst - slot_base, mode='drop')

        def migrate(k_layer, v_layer):
            outgoing = jnp.stack([k_layer[send_slot], v_layer[send_slot]], axis=1)
            incoming = lax.all_to_all(outgoing, 'kv', 0, 0, tiled=True)
            return k_layer.at[recv_slot].set(incoming[:, 0], mode='drop'), v_layer.at[recv_slot].set(incoming[:, 1], mode='drop')

        old_owner, old_page = slot_maps(old_table, False)
        new_owner, new_page = slot_maps(new_table, True)
        hid_zero = embeds[0]
        hid_one = embeds[1]
        k_layers = []
        v_layers = []
        for layer_idx in range(n_layers):
            k_layer = k_pool[:, layer_idx]
            v_layer = v_pool[:, layer_idx]
            query_rows, k_new, v_new = project_all(hid_zero, layer_idx)
            k_layer, v_layer = write_new(k_layer, v_layer, k_new, v_new, old_table, seq_len, False)
            hid_zero = finish_block(hid_zero, attend(query_rows, k_layer, v_layer, old_owner, old_page, seq_len), layer_idx)
            k_layer, v_layer = migrate(k_layer, v_layer)
            query_rows, k_new, v_new = project_all(hid_one, layer_idx)
            k_layer, v_layer = write_new(k_layer, v_layer, k_new, v_new, new_table, len_next, True)
            hid_one = finish_block(hid_one, attend(query_rows, k_layer, v_layer, new_owner, new_page, len_next), layer_idx)
            k_layers.append(k_layer)
            v_layers.append(v_layer)
        hid_one = jnp.where(home_done[:, None] == 0, hid_one, jnp.zeros_like(hid_one))
        return jnp.stack([hid_zero, hid_one]), jnp.stack(k_layers, axis=1), jnp.stack(v_layers, axis=1)

    in_specs = (rows_spec, full_spec, full_spec, full_spec, full_spec, full_spec, full_spec, pool_spec, pool_spec, table_spec, table_spec, vec_spec, vec_spec, vec_spec, vec_spec)
    return jax.shard_map(device_fn, mesh=mesh, in_specs=in_specs, out_specs=(rows_spec, pool_spec, pool_spec), check_vma=False)
```

profile of v0, /device:TPU:97, one launch (start us, length us, event | category | flops | bytes accessed | tf_op | source)
XLA Modules:
  0.0 994.5 jit_solution(2481031157433122916)
XLA Ops:
  38.1 6.7 scatter_custom_fusion.1
  44.9 11.0 %slice_bitcast_fusion.5 = (bf16[72,16,16,128]{3,2,1,0:T(8,128)(2,1)}, bf16[72,16,16,128]{3,2,1,0:T(8,128)(2,1)}) fusion(bf16[72,2,16,16,128]{4,3,2,1,0:T(8,128)(2,1)} %param.26), kind=kLoop, calls=%fused_computation.150 | loop fusion | bytes 18874368 | tf_op jit(solution)/shard_map/squeeze | solution.py:120
  55.8 10.9 %slice_bitcast_fusion.4 = (bf16[72,16,16,128]{3,2,1,0:T(8,128)(2,1)}, bf16[72,16,16,128]{3,2,1,0:T(8,128)(2,1)}) fusion(bf16[72,2,16,16,128]{4,3,2,1,0:T(8,128)(2,1)} %param.27), kind=kLoop, calls=%fused_computation.149 | loop fusion | bytes 18874368 | tf_op jit(solution)/shard_map/squeeze | solution.py:121
  71.0 11.5 %scatter_fusion = bf16[72,16,16,128]{3,2,1,0:T(8,128)(2,1)} fusion(bf16[72,16,16,128]{3,2,1,0:T(8,128)(2,1)} %get-tuple-element.114, s32[128]{0:T(128)S(1)} %fusion.328, bf16[128,16,128]{2,1,0:T(8,128)(2,1)S(1)} %bitcast.494), kind=kCustom, calls=%fused_computation.20 | custom fusion | bytes 1573888 | tf_op jit(solution)/shard_map/scatter | solution.py:61
  93.7 12.8 %all-to-all-start.1 = ((f32[32,1,128]{2,1,0:T(1,128)}), f32[32,1,128]{2,1,0:T(1,128)S(1)}, u32[]{:S(2)}, u32[]{:S(2)}) async-start(f32[32,1,128]{2,1,0:T(1,128)} %reshape.1431), calls=%async_computation.1 | async-start | bytes 32768 | tf_op jit(solution)/shard_map/all_to_all | solution.py:64
  106.4 11.4 %scatter_fusion.1 = bf16[72,16,16,128]{3,2,1,0:T(8,128)(2,1)} fusion(bf16[72,16,16,128]{3,2,1,0:T(8,128)(2,1)} %get-tuple-element.112, s32[128]{0:T(128)S(1)} %fusion.328, bf16[128,16,128]{2,1,0:T(8,128)(2,1)S(1)} %bitcast.490), kind=kCustom, calls=%fused_computation.21 | custom fusion | bytes 1573888 | tf_op jit(solution)/shard_map/scatter | solution.py:61
  122.9 10.3 %scatter_fusion.2 = f32[128,16,128]{2,1,0:T(8,128)} fusion(f32[128,16,128]{2,1,0:T(8,128)} %broadcast.624.clone.2, s32[72]{0:T(128)S(1)} %scatter_custom_fusion, f32[72,16,128]{2,1,0:T(8,128)S(1)} %broadcast_multiply_fusion.3), kind=kCustom, calls=%fused_computation.23 | custom fusion | flops 147456 | bytes 1769760 | tf_op jit(solution)/shard_map/scatter-add | solution.py:80
  133.2 8.1 all-to-all-start
  142.5 15.3 %all-to-all-done = f32[128,16,1,128]{3,1,2,0:T(8,128)S(1)} async-done(((f32[128,16,1,128]{3,1,2,0:T(8,128)}), f32[128,16,1,128]{3,1,2,0:T(8,128)S(1)}, u32[]{:S(2)}, u32[]{:S(2)}) %all-to-all-start) | async-done | bytes 1048608 | tf_op jit(solution)/shard_map/all_to_all | solution.py:64
  162.8 22.7 %fusion.121 = bf16[4,2048]{1,0:T(4,128)(2,1)S(1)} fusion(bf16[2,8192,2048]{2,1,0:T(8,128)(2,1)} %param.25, bf16[4,2048]{1,0:T(4,128)(2,1)S(1)} %fusion.133, bf16[2,2048,8192]{2,1,0:T(8,128)(2,1)} %param.24), kind=kOutput, calls=%fused_computation.164 | convolution fusion | flops 268754944 | bytes 67158016 | tf_op jit(solution)/shard_map/dot_general | solution.py:94
  200.0 32.8 %while.25 = (s32[]{:T(128)}, u32[768]{0:T(1024)S(1)}, u32[768]{0:T(1024)S(1)}, s32[768]{0:T(1024)S(1)}, s32[]{:T(128)}, /*index=5*/s32[]{:T(128)}, s32[]{}) while((s32[]{:T(128)}, u32[768]{0:T(1024)S(1)}, u32[768]{0:T(1024)S(1)}, s32[768]{0:T(1024)S(1)}, s32[]{:T(128)}, /*index=5*/s32[]{:T(128)}, s32[]{}) %tuple.70), condition=%wide.region_26.28_spmd.clone, body=%wide.region_25.27_spmd.clone.sunk | while | flops 14852 | bytes 57965 | solution.py:101
  239.9 8.2 gather_fusion.10
  248.1 8.2 gather_fusion.9
  260.4 11.4 %scatter_fusion.3 = bf16[72,16,16,128]{3,2,1,0:T(8,128)(2,1)} fusion(bf16[72,16,16,128]{3,2,1,0:T(8,128)(2,1)} %get-tuple-element.113, s32[128]{0:T(128)S(1)} %fusion.328, bf16[128,16,128]{2,1,0:T(8,128)(2,1)S(1)} %bitcast.493), kind=kCustom, calls=%fused_computation.25 | custom fusion | bytes 1573888 | tf_op jit(solution)/shard_map/scatter | solution.py:61
  288.1 10.5 %pad_maximum_fusion = bf16[96,2,16,16,128]{4,3,2,1,0:T(8,128)(2,1)} fusion(bf16[96,1,16,16,128]{4,3,2,1,0:T(8,128)(2,1)} %bitcast.476, bf16[96,1,16,16,128]{4,3,2,1,0:T(8,128)(2,1)} %bitcast.477), kind=kLoop, calls=%fused_computation.77 | loop fusion | flops 6291456 | bytes 25165824 | tf_op jit(solution)/shard_map/stack | solution.py:109
  298.6 6.4 all-to-all-start.4
  338.1 80.4 %all-gather.13.cloned.1.call-done = bf16[32,4,6144]{2,1,0:T(4,128)(2,1)} async-done(((bf16[1,4,6144]{2,1,0:T(4,128)(2,1)}), bf16[32,4,6144]{2,1,0:T(4,128)(2,1)}) %all-gather.13.cloned.1.call-update) | async-done | bytes 1572880 | tf_op jit(solution)/shard_map/all_gather | solution.py:47
  425.3 8.2 gather_fusion.13
  433.6 11.3 %scatter_fusion.4 = bf16[72,16,16,128]{3,2,1,0:T(8,128)(2,1)} fusion(bf16[72,16,16,128]{3,2,1,0:T(8,128)(2,1)} %get-tuple-element.111, s32[128]{0:T(128)S(1)} %fusion.328, bf16[128,16,128]{2,1,0:T(8,128)(2,1)S(1)} %bitcast.492), kind=kCustom, calls=%fused_computation.26 | custom fusion | bytes 1573888 | tf_op jit(solution)/shard_map/scatter | solution.py:61
  445.0 8.2 gather_fusion.14
  458.9 10.3 %scatter_fusion.5 = f32[128,16,128]{2,1,0:T(8,128)} fusion(f32[128,16,128]{2,1,0:T(8,128)} %broadcast.624.clone.3, s32[72]{0:T(128)S(1)} %scatter_custom_fusion, f32[72,16,128]{2,1,0:T(8,128)S(1)} %broadcast_multiply_fusion.2), kind=kCustom, calls=%fused_computation.28 | custom fusion | flops 147456 | bytes 1769760 | tf_op jit(solution)/shard_map/scatter-add | solution.py:80
  469.2 10.4 %pad_maximum_fusion.1 = bf16[96,2,16,16,128]{4,3,2,1,0:T(8,128)(2,1)} fusion(bf16[96,1,16,16,128]{4,3,2,1,0:T(8,128)(2,1)} %bitcast.479, bf16[96,1,16,16,128]{4,3,2,1,0:T(8,128)(2,1)} %bitcast.478), kind=kLoop, calls=%fused_computation.78 | loop fusion | flops 6291456 | bytes 25165824 | tf_op jit(solution)/shard_map/stack | solution.py:109
  480.7 34.6 %all-to-all-start.2 = ((f32[128,16,1,128]{3,1,2,0:T(8,128)}), f32[128,16,1,128]{3,1,2,0:T(8,128)S(1)}, u32[]{:S(2)}, u32[]{:S(2)}) async-start(f32[128,16,1,128]{3,1,2,0:T(8,128)} %bitcast.40), calls=%async_computation.2 | async-start | bytes 2097152 | tf_op jit(solution)/shard_map/all_to_all | solution.py:64
  515.3 12.1 %slice_bitcast_fusion.2 = (bf16[96,16,16,128]{3,2,1,0:T(8,128)(2,1)}, bf16[96,16,16,128]{3,2,1,0:T(8,128)(2,1)}) fusion(bf16[96,2,16,16,128]{4,3,2,1,0:T(8,128)(2,1)} %all-to-all-done.4), kind=kLoop, calls=%fused_computation.131 | loop fusion | bytes 25165824 | tf_op jit(solution)/shard_map/squeeze | solution.py:111
  527.4 17.4 %scatter_fusion.6 = bf16[72,16,16,128]{3,2,1,0:T(8,128)(2,1)} fusion(bf16[72,16,16,128]{3,2,1,0:T(8,128)(2,1)} %scatter_fusion, s32[96]{0:T(128)S(1)} %compare_select_fusion.15, bf16[96,16,16,128]{3,2,1,0:T(8,128)(2,1)} %get-tuple-element.110), kind=kCustom, calls=%fused_computation.35 | custom fusion | bytes 18874752 | tf_op jit(solution)/shard_map/scatter | solution.py:111
  544.8 11.4 %scatter_fusion.7 = bf16[72,16,16,128]{3,2,1,0:T(8,128)(2,1)} fusion(bf16[72,16,16,128]{3,2,1,0:T(8,128)(2,1)} %scatter_fusion.6, s32[128]{0:T(128)S(1)} %get-tuple-element.148, bf16[128,16,128]{2,1,0:T(8,128)(2,1)S(1)} %bitcast.489), kind=kCustom, calls=%fused_computation.36 | custom fusion | bytes 1573888 | tf_op jit(solution)/shard_map/scatter | solution.py:61
  562.2 17.4 %scatter_fusion.8 = bf16[72,16,16,128]{3,2,1,0:T(8,128)(2,1)} fusion(bf16[72,16,16,128]{3,2,1,0:T(8,128)(2,1)} %scatter_fusion.1, s32[96]{0:T(128)S(1)} %compare_select_fusion.15, bf16[96,16,16,128]{3,2,1,0:T(8,128)(2,1)} %get-tuple-element.109), kind=kCustom, calls=%fused_computation.37 | custom fusion | bytes 18874752 | tf_op jit(solution)/shard_map/scatter | solution.py:111
  584.2 11.4 %scatter_fusion.9 = bf16[72,16,16,128]{3,2,1,0:T(8,128)(2,1)} fusion(bf16[72,16,16,128]{3,2,1,0:T(8,128)(2,1)} %scatter_fusion.8, s32[128]{0:T(128)S(1)} %get-tuple-element.148, bf16[128,16,128]{2,1,0:T(8,128)(2,1)S(1)} %bitcast.488), kind=kCustom, calls=%fused_computation.38 | custom fusion | bytes 1573888 | tf_op jit(solution)/shard_map/scatter | solution.py:61
  599.4 9.5 all-to-all-start.6
  610.2 9.2 scatter_fusion.10
  619.4 6.9 all-to-all-start.5
  626.8 16.0 %all-to-all-done.5 = f32[128,16,1,128]{3,1,2,0:T(8,128)S(1)} async-done(((f32[128,16,1,128]{3,1,2,0:T(8,128)}), f32[128,16,1,128]{3,1,2,0:T(8,128)S(1)}, u32[]{:S(2)}, u32[]{:S(2)}) %all-to-all-start.5) | async-done | bytes 1048608 | tf_op jit(solution)/shard_map/all_to_all | solution.py:64
  658.4 23.1 %fusion.118 = bf16[4,2048]{1,0:T(4,128)(2,1)S(1)} fusion(bf16[2,8192,2048]{2,1,0:T(8,128)(2,1)} %param.25, bf16[4,2048]{1,0:T(4,128)(2,1)S(1)} %fusion.130, bf16[2,2048,8192]{2,1,0:T(8,128)(2,1)} %param.24), kind=kOutput, calls=%fused_computation.163 | convolution fusion | flops 268754944 | bytes 67158016 | tf_op jit(solution)/shard_map/dot_general | solution.py:94
  696.0 22.7 %fusion.172 = bf16[1,4,2048]{2,1,0:T(4,128)(2,1)S(1)} fusion(bf16[2,8192,2048]{2,1,0:T(8,128)(2,1)} %param.25, bf16[4,2048]{1,0:T(4,128)(2,1)S(1)} %fusion.127, bf16[2,2048,8192]{2,1,0:T(8,128)(2,1)} %param.24), kind=kOutput, calls=%fused_computation.181 | convolution fusion | flops 268754944 | bytes 67158016 | tf_op jit(solution)/shard_map/dot_general | solution.py:94
  718.7 74.4 %all-gather.15.cloned.1.call-done = bf16[32,4,6144]{2,1,0:T(4,128)(2,1)} async-done(((bf16[1,4,6144]{2,1,0:T(4,128)(2,1)}), bf16[32,4,6144]{2,1,0:T(4,128)(2,1)}) %all-gather.15.cloned.1.call-update) | async-done | bytes 1572880 | tf_op jit(solution)/shard_map/all_gather | solution.py:47
  797.2 15.5 %all-to-all-done.7 = bf16[96,2,16,16,128]{4,3,2,1,0:T(8,128)(2,1)} async-done(((bf16[96,2,16,16,128]{4,3,2,1,0:T(8,128)(2,1)}), bf16[96,2,16,16,128]{4,3,2,1,0:T(8,128)(2,1)}, u32[]{:S(2)}, u32[]{:S(2)}) %all-to-all-start.7) | async-done | bytes 12582944 | tf_op jit(solution)/shard_map/all_to_all | solution.py:110
  812.7 12.0 %slice_bitcast_fusion = (bf16[96,16,16,128]{3,2,1,0:T(8,128)(2,1)}, bf16[96,16,16,128]{3,2,1,0:T(8,128)(2,1)}) fusion(bf16[96,2,16,16,128]{4,3,2,1,0:T(8,128)(2,1)} %all-to-all-done.7), kind=kLoop, calls=%fused_computation.129 | loop fusion | bytes 25165824 | tf_op jit(solution)/shard_map/squeeze | solution.py:111
  824.7 17.6 %scatter_fusion.11 = bf16[72,16,16,128]{3,2,1,0:T(8,128)(2,1)} fusion(bf16[72,16,16,128]{3,2,1,0:T(8,128)(2,1)} %scatter_fusion.3, s32[96]{0:T(128)S(1)} %compare_select_fusion.15, bf16[96,16,16,128]{3,2,1,0:T(8,128)(2,1)} %get-tuple-element.108), kind=kCustom, calls=%fused_computation.42 | custom fusion | bytes 18874752 | tf_op jit(solution)/shard_map/scatter | solution.py:111
  842.4 11.6 %scatter_fusion.12 = bf16[72,16,16,128]{3,2,1,0:T(8,128)(2,1)} fusion(bf16[72,16,16,128]{3,2,1,0:T(8,128)(2,1)} %scatter_fusion.11, s32[128]{0:T(128)S(1)} %get-tuple-element.148, bf16[128,16,128]{2,1,0:T(8,128)(2,1)S(1)} %bitcast.495), kind=kCustom, calls=%fused_computation.43 | custom fusion | bytes 1573888 | tf_op jit(solution)/shard_map/scatter | solution.py:61
  860.0 17.5 %scatter_fusion.13 = bf16[72,16,16,128]{3,2,1,0:T(8,128)(2,1)} fusion(bf16[72,16,16,128]{3,2,1,0:T(8,128)(2,1)} %scatter_fusion.4, s32[96]{0:T(128)S(1)} %compare_select_fusion.15, bf16[96,16,16,128]{3,2,1,0:T(8,128)(2,1)} %get-tuple-element.107), kind=kCustom, calls=%fused_computation.44 | custom fusion | bytes 18874752 | tf_op jit(solution)/shard_map/scatter | solution.py:111
  882.2 11.3 %all-to-all-start.9 = ((f32[32,1,128]{2,1,0:T(1,128)}), f32[32,1,128]{2,1,0:T(1,128)S(1)}, u32[]{:S(2)}, u32[]{:S(2)}) async-start(f32[32,1,128]{2,1,0:T(1,128)} %reshape.1433), calls=%async_computation.9 | async-start | bytes 32768 | tf_op jit(solution)/shard_map/all_to_all | solution.py:64
  893.6 11.3 %scatter_fusion.14 = bf16[72,16,16,128]{3,2,1,0:T(8,128)(2,1)} fusion(bf16[72,16,16,128]{3,2,1,0:T(8,128)(2,1)} %scatter_fusion.13, s32[128]{0:T(128)S(1)} %get-tuple-element.148, bf16[128,16,128]{2,1,0:T(8,128)(2,1)S(1)} %bitcast.491), kind=kCustom, calls=%fused_computation.45 | custom fusion | bytes 1573888 | tf_op jit(solution)/shard_map/scatter | solution.py:61
  908.7 8.4 pad_maximum_fusion.2
  917.1 8.4 pad_maximum_fusion.3
  926.7 9.2 scatter_fusion.15
  936.0 7.5 all-to-all-start.8
  944.7 14.7 %all-to-all-done.8 = f32[128,16,1,128]{3,1,2,0:T(8,128)S(1)} async-done(((f32[128,16,1,128]{3,1,2,0:T(8,128)}), f32[128,16,1,128]{3,1,2,0:T(8,128)S(1)}, u32[]{:S(2)}, u32[]{:S(2)}) %all-to-all-start.8) | async-done | bytes 1048608 | tf_op jit(solution)/shard_map/all_to_all | solution.py:64
  964.4 22.7 %fusion.178 = bf16[1,4,2048]{2,1,0:T(4,128)(2,1)S(1)} fusion(bf16[2,8192,2048]{2,1,0:T(8,128)(2,1)} %param.25, bf16[4,2048]{1,0:T(4,128)(2,1)S(1)} %fusion.124, bf16[2,2048,8192]{2,1,0:T(8,128)(2,1)} %param.24, pred[4]{0:T(512)(128)(4,1)S(1)} %copy-done.9), kind=kOutput, calls=%fused_computation.183 | convolution fusion | flops 268763136 | bytes 67158528 | tf_op jit(solution)/shard_map/dot_general | solution.py:94
  (323 shorter events, 250.3 us)
Async XLA Ops:
  7.2 4.8 copy-start.5
  7.2 59.6 %all-gather.9.cloned.1.call-start = ((), (), s32[]{:S(2)}) async-start(), calls=%async_computation.10 | async-start | bytes 1622016 | tf_op jit(solution)/shard_map/all_gather | solution.py:47
  7.3 10.6 %copy-start.1 = (bf16[2,2048,2048]{2,1,0:T(8,128)(2,1)S(1)}, bf16[2,2048,2048]{2,1,0:T(8,128)(2,1)}, u32[]{:S(2)}) copy-start(bf16[2,2048,2048]{2,1,0:T(8,128)(2,1)} %param.20) | copy-start | bytes 50331652
  17.8 2.0 copy-start.8
  17.8 2.1 copy-start.2
  17.8 2.1 copy-start.3
  17.8 2.4 copy-start
  17.8 5.1 copy-start.6
  17.8 5.1 copy-start.7
  93.7 39.5 %all-to-all-start.1 = ((f32[32,1,128]{2,1,0:T(1,128)}), f32[32,1,128]{2,1,0:T(1,128)S(1)}, u32[]{:S(2)}, u32[]{:S(2)}) async-start(f32[32,1,128]{2,1,0:T(1,128)} %reshape.1431), calls=%async_computation.1 | async-start | bytes 32768 | tf_op jit(solution)/shard_map/all_to_all | solution.py:64
  133.2 24.7 %all-to-all-start = ((f32[128,16,1,128]{3,1,2,0:T(8,128)}), f32[128,16,1,128]{3,1,2,0:T(8,128)S(1)}, u32[]{:S(2)}, u32[]{:S(2)}) async-start(f32[128,16,1,128]{3,1,2,0:T(8,128)} %bitcast.18), calls=%async_computation | async-start | bytes 2097152 | tf_op jit(solution)/shard_map/all_to_all | solution.py:64
  141.3 115.0 %all-gather.11.cloned.1.call-start = ((), (), s32[]{:S(2)}) async-start(), calls=%async_computation.11 | async-start | bytes 1622016 | tf_op jit(solution)/shard_map/all_gather | solution.py:47
  281.8 16.8 %all-to-all-start.3 = ((f32[32,1,128]{2,1,0:T(1,128)}), f32[32,1,128]{2,1,0:T(1,128)S(1)}, u32[]{:S(2)}, u32[]{:S(2)}) async-start(f32[32,1,128]{2,1,0:T(1,128)} %reshape.1435), calls=%async_computation.3 | async-start | bytes 32768 | tf_op jit(solution)/shard_map/all_to_all | solution.py:64
  298.6 182.1 %all-to-all-start.4 = ((bf16[96,2,16,16,128]{4,3,2,1,0:T(8,128)(2,1)}), bf16[96,2,16,16,128]{4,3,2,1,0:T(8,128)(2,1)}, u32[]{:S(2)}, u32[]{:S(2)}) async-start(bf16[96,2,16,16,128]{4,3,2,1,0:T(8,128)(2,1)} %pad_maximum_fusion), calls=%async_computation.4 | async-start | bytes 25165824 | tf_op jit(solution)/shard_map/all_to_all | solution.py:110
  305.0 113.4 %all-gather.13.cloned.1.call-start = ((), (), s32[]{:S(2)}) async-start(), calls=%async_computation.12 | async-start | bytes 1622016 | tf_op jit(solution)/shard_map/all_gather | solution.py:47
  480.7 118.7 %all-to-all-start.2 = ((f32[128,16,1,128]{3,1,2,0:T(8,128)}), f32[128,16,1,128]{3,1,2,0:T(8,128)S(1)}, u32[]{:S(2)}, u32[]{:S(2)}) async-start(f32[128,16,1,128]{3,1,2,0:T(8,128)} %bitcast.40), calls=%async_computation.2 | async-start | bytes 2097152 | tf_op jit(solution)/shard_map/all_to_all | solution.py:64
  527.4 28.9 %copy-start.4 = (bf16[72,16,128,1]{2,3,1,0:T(2,128)(2,1)S(1)}, bf16[72,16,128,1]{2,3,1,0:T(2,128)(2,1)}, u32[]{:S(2)}) copy-start(bf16[72,16,128,1]{2,3,1,0:T(2,128)(2,1)} %reshape.1394) | copy-start | bytes 884740
  599.4 20.0 %all-to-all-start.6 = ((f32[32,1,128]{2,1,0:T(1,128)}), f32[32,1,128]{2,1,0:T(1,128)S(1)}, u32[]{:S(2)}, u32[]{:S(2)}) async-start(f32[32,1,128]{2,1,0:T(1,128)} %reshape.1429), calls=%async_computation.6 | async-start | bytes 32768 | tf_op jit(solution)/shard_map/all_to_all | solution.py:64
  619.4 23.5 %all-to-all-start.5 = ((f32[128,16,1,128]{3,1,2,0:T(8,128)}), f32[128,16,1,128]{3,1,2,0:T(8,128)S(1)}, u32[]{:S(2)}, u32[]{:S(2)}) async-start(f32[128,16,1,128]{3,1,2,0:T(8,128)} %bitcast.72), calls=%async_computation.5 | async-start | bytes 2097152 | tf_op jit(solution)/shard_map/all_to_all | solution.py:64
  642.9 169.8 %all-to-all-start.7 = ((bf16[96,2,16,16,128]{4,3,2,1,0:T(8,128)(2,1)}), bf16[96,2,16,16,128]{4,3,2,1,0:T(8,128)(2,1)}, u32[]{:S(2)}, u32[]{:S(2)}) async-start(bf16[96,2,16,16,128]{4,3,2,1,0:T(8,128)(2,1)} %pad_maximum_fusion.1), calls=%async_computation.7 | async-start | bytes 25165824 | tf_op jit(solution)/shard_map/all_to_all | solution.py:110
  647.6 145.5 %all-gather.15.cloned.1.call-start = ((), (), s32[]{:S(2)}) async-start(), calls=%async_computation.13 | async-start | bytes 1622016 | tf_op jit(solution)/shard_map/all_gather | solution.py:47
  882.2 53.7 %all-to-all-start.9 = ((f32[32,1,128]{2,1,0:T(1,128)}), f32[32,1,128]{2,1,0:T(1,128)S(1)}, u32[]{:S(2)}, u32[]{:S(2)}) async-start(f32[32,1,128]{2,1,0:T(1,128)} %reshape.1433), calls=%async_computation.9 | async-start | bytes 32768 | tf_op jit(solution)/shard_map/all_to_all | solution.py:64
  936.0 28.4 %copy-start.9 = (pred[4]{0:T(512)(128)(4,1)S(1)}, pred[4]{0:T(512)(128)(4,1)}, u32[]{:S(2)}) copy-start(pred[4]{0:T(512)(128)(4,1)} %dynamic-slice_compare_fusion) | copy-start | bytes 16
  936.0 23.4 %all-to-all-start.8 = ((f32[128,16,1,128]{3,1,2,0:T(8,128)}), f32[128,16,1,128]{3,1,2,0:T(8,128)S(1)}, u32[]{:S(2)}, u32[]{:S(2)}) async-start(f32[128,16,1,128]{3,1,2,0:T(8,128)} %bitcast.90), calls=%async_computation.8 | async-start | bytes 2097152 | tf_op jit(solution)/shard_map/all_to_all | solution.py:64
Sparse Core Ops, SparseCore 0:
  19.9 42.0 all-gather.8
  200.1 36.4 all-gather.10
  320.1 98.3 all-gather.12
  696.1 96.9 all-gather.14
where the time goes:
time: 1010 us; the launch traced here: 994 us
  local copies, waits for them, and re-layouts  354 us (35%)
  waiting for transfers between devices  217 us (21%)
  matrix products  196 us (19%)
  starting transfers between devices  109 us (11%)
  other arithmetic  103 us (10%)
  between operations  15.4 us (2%)
    all_gather x4, waiting for transfers between devices, project_all(): gathered = lax.all_gather(packed, 'kv', axis=0, tiled=True)  155 us
    all_to_all x8, starting transfers between devices, to_home(): return lax.all_to_all(values, 'kv', 0, 0, tiled=True)  97 us
    dot_general x4, matrix products, finish_block(): jnp.dot(inner_act, w_down[layer_idx], preferred_element_type=jnp.float32)  91.1 us
    all_to_all x8, waiting for transfers between devices, to_home(): return lax.all_to_all(values, 'kv', 0, 0, tiled=True)  46 us
    scatter x4, local copies, waits for them, and re-layouts, write_new(): k_layer.at[write_rows, offset].set(k_new, mode='drop')  45.9 us
    scatter x4, local copies, waits for them, and re-layouts, write_new(): v_layer.at[write_rows, offset].set(v_new, mode='drop')  45.5 us
    scatter-add x4, other arithmetic, attend(): jax.ops.segment_sum(slot_out * factor[..., None], slot_owner, num_segment...  39 us
    scatter x2, local copies, waits for them, and re-layouts, migrate(): k_layer.at[recv_slot].set(incoming[:, 0], mode='drop')  35 us
  transfers between devices with their start and end apart: 14, of which 6 were waited for; matrix products, arithmetic and copies ran while one was open for 45% of the time, Pallas kernels for 0%

commit v1 on v0

v1 whole, which is shorter than its diff:
```python
import functools

import jax
import jax.numpy as jnp
from jax import lax
from jax.experimental import pallas as pl
from jax.experimental.pallas import tpu as pltpu
from jax.sharding import PartitionSpec as P

MESH = pl.DeviceIdType.MESH
ANY = pl.BlockSpec(memory_space=pl.ANY)
VMEM = pl.BlockSpec(memory_space=pltpu.VMEM)
SMEM = pl.BlockSpec(memory_space=pltpu.SMEM)
LOW = -1e30


def ring(count, depth, lead, start_in, wait_in, middle, start_out, wait_out):
    def body(i, carry):
        @pl.when(i < count)
        def _():
            @pl.when(i >= depth)
            def _():
                wait_out(i - depth)

            start_in(i)

        @pl.when(i >= lead)
        def _():
            wait_in(i - lead)
            middle(i - lead)
            start_out(i - lead)

        return carry

    lax.fori_loop(0, count + lead, body, 0)

    def drain(i, carry):
        wait_out(i)
        return carry

    lax.fori_loop(jnp.maximum(count - depth, 0), count, drain, 0)


def compact(total, flag, value, listed):
    def body(i, count):
        @pl.when(flag(i))
        def _():
            listed[count] = value(i)

        return count + flag(i).astype(jnp.int32)

    return lax.fori_loop(0, total, body, jnp.int32(0))


def pack_kernel(depth, lead, slot_ref, k_ref, v_ref, *rest):
    outs, (buf, listed, sems_in, sems_out) = rest[:-4], rest[-4:]
    peers = slot_ref.shape[0] // len(outs)
    for r, out in enumerate(outs):
        count = compact(peers, lambda i: slot_ref[r * peers + i] >= 0, lambda i: i, listed)

        def ins(i):
            at = lax.rem(i, depth)
            slot = slot_ref[r * peers + listed[i]]
            return [pltpu.make_async_copy(ref.at[slot], buf.at[at, h], sems_in.at[at, h]) for h, ref in enumerate((k_ref, v_ref))]

        def put(i):
            at = lax.rem(i, depth)
            return pltpu.make_async_copy(buf.at[at], out.at[listed[i]], sems_out.at[at])

        ring(
            count, depth, lead,
            lambda i: [c.start() for c in ins(i)],
            lambda i: [c.wait() for c in ins(i)],
            lambda i: None,
            lambda i: put(i).start(),
            lambda i: put(i).wait(),
        )


def pack_pages(send_slot, k_pool, v_pool, rounds, peers):
    page = k_pool.shape[1:]
    depth, lead = 16, 8
    return pl.pallas_call(
        functools.partial(pack_kernel, depth, lead),
        out_shape=[jax.ShapeDtypeStruct((peers, 2) + page, k_pool.dtype)] * rounds,
        in_specs=[SMEM, ANY, ANY],
        out_specs=[ANY] * rounds,
        scratch_shapes=[
            pltpu.VMEM((depth, 2) + page, k_pool.dtype),
            pltpu.SMEM((peers,), jnp.int32),
            pltpu.SemaphoreType.DMA((depth, 2)),
            pltpu.SemaphoreType.DMA((depth,)),
        ],
        name="pack_pages",
    )(send_slot, k_pool, v_pool)


def patch_rows(buf, at, slot, first_ref, second_ref, offset_ref, rows):
    seq_dev = rows[0].shape[2]
    for step, ref in enumerate((first_ref, second_ref)):
        seq = ref[slot]

        @pl.when(seq >= 0)
        def _():
            offset = offset_ref[seq] + step
            home, place = seq // seq_dev, lax.rem(seq, seq_dev)
            for layer, row in enumerate(rows):
                for h in range(2):
                    buf[at, h, layer, offset] = row[home, h, place, step]


def keep_kernel(depth, lead, from_ref, first_ref, second_ref, offset_ref, k_ref, v_ref, *rest):
    n_layers = k_ref.shape[1]
    rows = rest[:n_layers]
    k_out, v_out, buf, listed, sems_in, sems_out = rest[n_layers:]
    count = compact(from_ref.shape[0], lambda i: from_ref[i] < 0, lambda i: i, listed)

    def ins(i):
        at = lax.rem(i, depth)
        return [pltpu.make_async_copy(ref.at[listed[i]], buf.at[at, h], sems_in.at[at, h]) for h, ref in enumerate((k_ref, v_ref))]

    def outs(i):
        at = lax.rem(i, depth)
        return [pltpu.make_async_copy(buf.at[at, h], ref.at[listed[i]], sems_out.at[at, h]) for h, ref in enumerate((k_out, v_out))]

    ring(
        count, depth, lead,
        lambda i: [c.start() for c in ins(i)],
        lambda i: [c.wait() for c in ins(i)],
        lambda i: patch_rows(buf, lax.rem(i, depth), listed[i], first_ref, second_ref, offset_ref, rows),
        lambda i: [c.start() for c in outs(i)],
        lambda i: [c.wait() for c in outs(i)],
    )


def keep_pages(from_page, first_seq, second_seq, offsets, k_pool, v_pool, rows):
    depth, lead = 16, 8
    return pl.pallas_call(
        functools.partial(keep_kernel, depth, lead),
        out_shape=[jax.ShapeDtypeStruct(k_pool.shape, k_pool.dtype)] * 2,
        in_specs=[SMEM] * 4 + [ANY] * 2 + [VMEM] * len(rows),
        out_specs=[ANY] * 2,
        scratch_shapes=[
            pltpu.VMEM((depth, 2) + k_pool.shape[1:], k_pool.dtype),
            pltpu.SMEM((k_pool.shape[0],), jnp.int32),
            pltpu.SemaphoreType.DMA((depth, 2)),
            pltpu.SemaphoreType.DMA((depth, 2)),
        ],
        name="keep_pages",
    )(from_page, first_seq, second_seq, offsets, k_pool, v_pool, *rows)


def place_kernel(depth, lead, n_layers, rounds, from_ref, first_ref, second_ref, offset_ref, *rest):
    arrived = rest[:rounds]
    rows = rest[rounds:rounds + n_layers]
    k_out, v_out, buf, listed, sems_in, sems_out = rest[rounds + n_layers + 2:]
    peers = arrived[0].shape[0]
    for r in range(rounds):
        count = compact(
            from_ref.shape[0],
            lambda i: (from_ref[i] >= r * peers) & (from_ref[i] < (r + 1) * peers),
            lambda i: i,
            listed,
        )

        def take(i):
            at = lax.rem(i, depth)
            return pltpu.make_async_copy(arrived[r].at[from_ref[listed[i]] - r * peers], buf.at[at], sems_in.at[at])

        def outs(i):
            at = lax.rem(i, depth)
            return [pltpu.make_async_copy(buf.at[at, h], ref.at[listed[i]], sems_out.at[at, h]) for h, ref in enumerate((k_out, v_out))]

        ring(
            count, depth, lead,
            lambda i: take(i).start(),
            lambda i: take(i).wait(),
            lambda i: patch_rows(buf, lax.rem(i, depth), listed[i], first_ref, second_ref, offset_ref, rows),
            lambda i: [c.start() for c in outs(i)],
            lambda i: [c.wait() for c in outs(i)],
        )


def place_pages(from_page, first_seq, second_seq, offsets, arrived, rows, k_out, v_out):
    depth, lead = 16, 8
    rounds, n_layers = len(arrived), len(rows)
    first_pool = 4 + rounds + n_layers
    return pl.pallas_call(
        functools.partial(place_kernel, depth, lead, n_layers, rounds),
        out_shape=[jax.ShapeDtypeStruct(k_out.shape, k_out.dtype)] * 2,
        in_specs=[SMEM] * 4 + [ANY] * rounds + [VMEM] * n_layers + [ANY] * 2,
        out_specs=[ANY] * 2,
        scratch_shapes=[
            pltpu.VMEM((depth, 2) + k_out.shape[1:], k_out.dtype),
            pltpu.SMEM((k_out.shape[0],), jnp.int32),
            pltpu.SemaphoreType.DMA((depth,)),
            pltpu.SemaphoreType.DMA((depth, 2)),
        ],
        input_output_aliases={first_pool: 0, first_pool + 1: 1},
        name="place_pages",
    )(from_page, first_seq, second_seq, offsets, *arrived, *rows, k_out, v_out)


def attend_kernel(block, pages_seq, seq_dev, page_size, scale, code_ref, q_ref, k_ref, v_ref, acc_ref):
    rows, head_dim = q_ref.shape[-2:]
    heads = k_ref.shape[3]
    step = pl.program_id(0)

    @pl.when(step == 0)
    def _():
        acc_ref[:, :seq_dev] = jnp.zeros((acc_ref.shape[0], seq_dev, rows, head_dim), jnp.float32)
        lane = lax.broadcasted_iota(jnp.int32, (acc_ref.shape[0], 1, rows, head_dim), 3)
        acc_ref[:, seq_dev:] = jnp.where(lax.rem(lane, 2) == 0, LOW, 0.0)

    row = lax.broadcasted_iota(jnp.int32, (rows, page_size * heads), 0)
    column = lax.broadcasted_iota(jnp.int32, (rows, page_size * heads), 1)
    same_head = lax.rem(row, heads) == lax.rem(column, heads)
    position = column // heads
    lane = lax.broadcasted_iota(jnp.int32, (rows, head_dim), 1)
    for s in range(block):
        code = code_ref[step * block + s]

        @pl.when(code >= 0)
        def _():
            seen = lax.rem(code, 2 * page_size)
            seq = code // (2 * page_size * pages_seq)
            home, place = seq // seq_dev, lax.rem(seq, seq_dev)
            q = q_ref[lax.rem(home, 2), home // 2, place]
            keys = k_ref[s, 0].reshape(page_size * heads, head_dim)
            values = v_ref[s, 0].reshape(page_size * heads, head_dim)
            scores = lax.dot_general(q, keys, (((1,), (1,)), ((), ())), preferred_element_type=jnp.float32) * scale
            mask = same_head & (position < seen)
            scores = jnp.where(mask, scores, LOW)
            top = jnp.max(scores, axis=1, keepdims=True)
            stats = acc_ref[home, seq_dev]
            old_top = jnp.max(jnp.where(lane == 2 * place, stats, LOW), axis=1, keepdims=True)
            old_sum = jnp.sum(jnp.where(lane == 2 * place + 1, stats, 0.0), axis=1, keepdims=True)
            new_top = jnp.maximum(top, old_top)
            weights = jnp.where(mask, jnp.exp(scores - new_top), 0.0)
            factor = jnp.exp(old_top - new_top)
            new_sum = old_sum * factor + jnp.sum(weights, axis=1, keepdims=True)
            high = weights.astype(jnp.bfloat16)
            low = (weights - high.astype(jnp.float32)).astype(jnp.bfloat16)
            mixed = jnp.dot(high, values, preferred_element_type=jnp.float32) + jnp.dot(low, values, preferred_element_type=jnp.float32)
            acc_ref[home, place] = acc_ref[home, place] * factor + mixed
            acc_ref[home, seq_dev] = jnp.where(lane == 2 * place, new_top, jnp.where(lane == 2 * place + 1, new_sum, stats))


def attend_pages(code, q_all, k_pool, v_pool, layer, pages_seq, seq_dev):
    slots, _, page_size, heads, head_dim = k_pool.shape
    rows = q_all.shape[-2]
    groups = q_all.shape[0] * q_all.shape[1]
    block = 8
    page_spec = pl.BlockSpec((block, 1, page_size, heads, head_dim), lambda i, c: (i, layer, 0, 0, 0))
    acc_shape = (groups, seq_dev + 1, rows, head_dim)
    return pl.pallas_call(
        functools.partial(attend_kernel, block, pages_seq, seq_dev, page_size, head_dim ** -0.5),
        out_shape=jax.ShapeDtypeStruct(acc_shape, jnp.float32),
        grid_spec=pltpu.PrefetchScalarGridSpec(
            num_scalar_prefetch=1,
            grid=(slots // block,),
            in_specs=[pl.BlockSpec(q_all.shape, lambda i, c: (0,) * q_all.ndim), page_spec, page_spec],
            out_specs=pl.BlockSpec(acc_shape, lambda i, c: (0, 0, 0, 0)),
        ),
        compiler_params=pltpu.CompilerParams(dimension_semantics=("arbitrary",)),
        cost_estimate=pl.CostEstimate(flops=4 * 10 ** 8, bytes_accessed=2 * slots * page_size * heads * head_dim * 2, transcendentals=0),
        name="attend_pages",
    )(code, q_all, k_pool, v_pool)


def spread_kernel(n, x_ref, out_ref, held, send_sem, recv_sem, pass_sem, got_sem, copy_sem):
    me = lax.axis_index("kv")
    chips = n // 2
    core, chip = lax.rem(me, 2), me // 2
    other = me + 1 - 2 * core

    def peer(j):
        return 2 * lax.rem(chip + j, chips) + core

    barrier = pltpu.get_barrier_semaphore()

    def greet(j, carry):
        pl.semaphore_signal(barrier, inc=1, device_id={"kv": peer(j)}, device_id_type=MESH)
        return carry

    lax.fori_loop(1, chips, greet, 0)
    pl.semaphore_signal(barrier, inc=1, device_id={"kv": other}, device_id_type=MESH)
    pl.semaphore_wait(barrier, chips)

    def send(j):
        return pltpu.make_async_remote_copy(
            src_ref=x_ref, dst_ref=held.at[core, chip], send_sem=send_sem.at[j], recv_sem=recv_sem.at[chip],
            device_id={"kv": peer(j)}, device_id_type=MESH,
        )

    def forward(source, at):
        return pltpu.make_async_remote_copy(
            src_ref=source, dst_ref=held.at[core, at], send_sem=pass_sem.at[at], recv_sem=got_sem.at[at],
            device_id={"kv": other}, device_id_type=MESH,
        )

    def start(j, carry):
        send(j).start()
        return carry

    lax.fori_loop(1, chips, start, 0)
    own = forward(x_ref, chip)
    own.start()
    mine = pltpu.make_async_copy(x_ref, out_ref.at[core, chip], copy_sem.at[0])
    mine.start()

    def arrive(j, carry):
        at = lax.rem(chip + chips - j, chips)
        pltpu.make_async_remote_copy(
            src_ref=x_ref, dst_ref=held.at[core, at], send_sem=send_sem.at[j], recv_sem=recv_sem.at[at],
            device_id={"kv": other}, device_id_type=MESH,
        ).wait_recv()
        forward(held.at[core, at], at).start()
        pltpu.make_async_copy(held.at[core, at], out_ref.at[core, at], copy_sem.at[j]).start()
        return carry

    lax.fori_loop(1, chips, arrive, 0)

    def passed(j, carry):
        at = lax.rem(chip + j, chips)
        pltpu.make_async_remote_copy(
            src_ref=x_ref, dst_ref=held.at[1 - core, at], send_sem=pass_sem.at[at], recv_sem=got_sem.at[at],
            device_id={"kv": other}, device_id_type=MESH,
        ).wait_recv()
        pltpu.make_async_copy(held.at[1 - core, at], out_ref.at[1 - core, at], copy_sem.at[chips + j]).start()
        return carry

    lax.fori_loop(0, chips, passed, 0)

    own.wait_send()
    mine.wait()

    def finish(j, carry):
        at = lax.rem(chip + chips - j, chips)
        send(j).wait_send()
        forward(held.at[core, at], at).wait_send()
        pltpu.make_async_copy(held.at[core, at], out_ref.at[core, at], copy_sem.at[j]).wait()
        return carry

    lax.fori_loop(1, chips, finish, 0)

    def written(j, carry):
        at = lax.rem(chip + j, chips)
        pltpu.make_async_copy(held.at[1 - core, at], out_ref.at[1 - core, at], copy_sem.at[chips + j]).wait()
        return carry

    lax.fori_loop(0, chips, written, 0)


def spread(x, n):
    chips = n // 2
    return pl.pallas_call(
        functools.partial(spread_kernel, n),
        out_shape=jax.ShapeDtypeStruct((2, chips) + x.shape, x.dtype),
        in_specs=[VMEM],
        out_specs=ANY,
        scratch_shapes=[
            pltpu.VMEM((2, chips) + x.shape, x.dtype),
            pltpu.SemaphoreType.DMA((chips,)),
            pltpu.SemaphoreType.DMA((chips,)),
            pltpu.SemaphoreType.DMA((chips,)),
            pltpu.SemaphoreType.DMA((chips,)),
            pltpu.SemaphoreType.DMA((n,)),
        ],
        compiler_params=pltpu.CompilerParams(collective_id=0, has_side_effects=True),
        name="spread_queries",
    )(x)


def gather_home_kernel(n, scale, acc_ref, q_ref, k_ref, v_ref, o_ref, held, send_sem, recv_sem):
    me = lax.axis_index("kv")
    seq_dev, rows, head_dim = q_ref.shape
    heads = k_ref.shape[2]

    def peer(j):
        return lax.rem(me + j, n)

    barrier = pltpu.get_barrier_semaphore()

    def greet(j, carry):
        pl.semaphore_signal(barrier, inc=1, device_id={"kv": peer(j)}, device_id_type=MESH)
        return carry

    lax.fori_loop(1, n, greet, 0)
    pl.semaphore_wait(barrier, n - 1)

    def send(j):
        return pltpu.make_async_remote_copy(
            src_ref=acc_ref.at[peer(j)], dst_ref=held.at[me], send_sem=send_sem.at[j], recv_sem=recv_sem.at[me],
            device_id={"kv": peer(j)}, device_id_type=MESH,
        )

    def start(j, carry):
        send(j).start()
        return carry

    lax.fori_loop(1, n, start, 0)
    held[me] = acc_ref[me]

    queries = [q_ref[i].astype(jnp.float32) for i in range(seq_dev)]
    second_row = lax.broadcasted_iota(jnp.int32, (rows, 1), 0) >= heads

    def twice(x):
        x = x.astype(jnp.float32)
        return jnp.concatenate([x, x], axis=0)

    first = [jnp.sum(queries[i] * twice(k_ref[i, 0]), axis=1, keepdims=True) * scale for i in range(seq_dev)]
    second = [
        jnp.where(second_row, jnp.sum(queries[i] * twice(k_ref[i, 1]), axis=1, keepdims=True) * scale, LOW)
        for i in range(seq_dev)
    ]

    def arrive(j, carry):
        at = lax.rem(me + n - j, n)
        pltpu.make_async_remote_copy(
            src_ref=acc_ref.at[at], dst_ref=held.at[at], send_sem=send_sem.at[j], recv_sem=recv_sem.at[at],
            device_id={"kv": peer(j)}, device_id_type=MESH,
        ).wait_recv()
        return carry

    lax.fori_loop(1, n, arrive, 0)

    def highest(j, top):
        return jnp.maximum(top, held[j, seq_dev])

    top_all = lax.fori_loop(0, n, highest, jnp.full((rows, head_dim), LOW, jnp.float32))
    tops, sums, mixed = [], [], []
    for i in range(seq_dev):
        top = jnp.maximum(jnp.maximum(top_all[:, 2 * i:2 * i + 1], first[i]), second[i])
        p_first, p_second = jnp.exp(first[i] - top), jnp.exp(second[i] - top)
        tops.append(top)
        sums.append(p_first + p_second)
        mixed.append(p_first * twice(v_ref[i, 0]) + p_second * twice(v_ref[i, 1]))

    def merge(j, carry):
        sums, mixed = carry
        stats = held[j, seq_dev]
        new_sums, new_mixed = [], []
        for i in range(seq_dev):
            weight = jnp.exp(stats[:, 2 * i:2 * i + 1] - tops[i])
            new_sums.append(sums[i] + weight * stats[:, 2 * i + 1:2 * i + 2])
            new_mixed.append(mixed[i] + weight * held[j, i])
        return tuple(new_sums), tuple(new_mixed)

    sums, mixed = lax.fori_loop(0, n, merge, (tuple(sums), tuple(mixed)))
    for i in range(seq_dev):
        o_ref[i] = (mixed[i] / sums[i]).astype(o_ref.dtype)

    def finish(j, carry):
        send(j).wait_send()
        return carry

    lax.fori_loop(1, n, finish, 0)


def gather_home(acc, q, k_new, v_new, n):
    return pl.pallas_call(
        functools.partial(gather_home_kernel, n, q.shape[-1] ** -0.5),
        out_shape=jax.ShapeDtypeStruct(q.shape, jnp.bfloat16),
        in_specs=[VMEM] * 4,
        out_specs=VMEM,
        scratch_shapes=[
            pltpu.VMEM(acc.shape, acc.dtype),
            pltpu.SemaphoreType.DMA((n,)),
            pltpu.SemaphoreType.DMA((n,)),
        ],
        compiler_params=pltpu.CompilerParams(collective_id=1, has_side_effects=True),
        name="gather_home",
    )(acc, q, k_new, v_new)


def solution(mesh):
    groups = mesh.shape['kv']
    rows_spec = P(None, ('rep', 'kv'), None)
    pool_spec = P(('rep', 'kv'))
    table_spec = P('rep', None)
    vec_spec = P('rep')
    full_spec = P()

    def device_fn(embeds, w_query, w_key, w_value, w_out, w_up, w_down, k_pool, v_pool, old_table, new_table, seq_len, finished, mig_src, mig_dst):
        me = lax.axis_index('kv')
        slots, n_layers, page_size, heads, head_dim = k_pool.shape
        steps, seq_dev, width = embeds.shape
        n_batch, pages_seq = old_table.shape
        n_mig = mig_src.shape[0]
        rounds = 4 * n_mig // (groups * groups)
        base = me * slots
        local = jnp.arange(slots, dtype=jnp.int32)
        active = finished == 0
        last = pages_seq - 1

        def find(match, value):
            return jnp.max(jnp.where(match, value, -1), axis=1)

        flat = old_table.reshape(-1)
        place = jnp.arange(n_batch * pages_seq, dtype=jnp.int32)
        seen = jnp.clip(seq_len[:, None] - jnp.arange(pages_seq, dtype=jnp.int32)[None, :] * page_size, 0, page_size).reshape(-1)
        code = find(flat[None, :] - base == local[:, None], (place * (2 * page_size) + seen)[None, :])

        src_dev, dst_dev = mig_src // slots, mig_dst // slots
        pair = src_dev * groups + dst_dev
        entry = jnp.arange(n_mig, dtype=jnp.int32)
        rank = jnp.sum((pair[None, :] == pair[:, None]) & (entry[None, :] < entry[:, None]), axis=1, dtype=jnp.int32)
        lines = jnp.arange(rounds * groups, dtype=jnp.int32)
        send_slot = find(
            ((rank * groups + dst_dev)[None, :] == lines[:, None]) & (src_dev == me)[None, :], (mig_src - src_dev * slots)[None, :]
        )
        from_page = find((mig_dst - base)[None, :] == local[:, None], (rank * groups + src_dev)[None, :])

        seq_ids = jnp.arange(n_batch, dtype=jnp.int32)
        owner_old = find((old_table[:, last] - base)[None, :] == local[:, None], seq_ids[None, :])
        owner_new = find(((new_table[:, last] - base)[None, :] == local[:, None]) & active[None, :], seq_ids[None, :])
        first_seq = jnp.where(from_page >= 0, owner_new, owner_old)
        second_seq = owner_new
        offsets = lax.rem(seq_len, page_size)

        packed = pack_pages(send_slot, k_pool, v_pool, rounds, groups)

        def exchange(block):
            return lax.all_to_all(block, 'kv', 0, 0, tiled=True)

        hidden = jnp.transpose(embeds, (1, 0, 2)).reshape(seq_dev * steps, width)
        arrived = []
        rows = []
        for layer in range(n_layers):
            query = jnp.dot(hidden, w_query[layer], preferred_element_type=jnp.float32).astype(jnp.bfloat16)
            key = jnp.dot(hidden, w_key[layer], preferred_element_type=jnp.float32).astype(jnp.bfloat16)
            value = jnp.dot(hidden, w_value[layer], preferred_element_type=jnp.float32).astype(jnp.bfloat16)
            query = query.reshape(seq_dev, steps * heads, head_dim)
            key = key.reshape(seq_dev, steps, heads, head_dim)
            value = value.reshape(seq_dev, steps, heads, head_dim)
            q_all = spread(query, groups)
            if layer == 0:
                block, q_all = lax.optimization_barrier((packed[0], q_all))
                arrived.append(exchange(block))
            acc = attend_pages(code, q_all, k_pool, v_pool, layer, pages_seq, seq_dev)
            mixed = gather_home(acc, query, key, value, groups)
            if layer + 1 < rounds:
                block, mixed = lax.optimization_barrier((packed[layer + 1], mixed))
                arrived.append(exchange(block))
            rows.append(lax.all_gather(jnp.stack([key, value])[None], 'kv', axis=0, tiled=True))
            mixed = mixed.reshape(seq_dev * steps, heads * head_dim)
            hidden = (hidden.astype(jnp.float32) + jnp.dot(mixed, w_out[layer], preferred_element_type=jnp.float32)).astype(jnp.bfloat16)
            inner = jax.nn.gelu(jnp.dot(hidden, w_up[layer], preferred_element_type=jnp.float32)).astype(jnp.bfloat16)
            hidden = (hidden.astype(jnp.float32) + jnp.dot(inner, w_down[layer], preferred_element_type=jnp.float32)).astype(jnp.bfloat16)
        for r in range(len(arrived), rounds):
            arrived.append(exchange(packed[r]))
        k_out, v_out = keep_pages(from_page, first_seq, second_seq, offsets, k_pool, v_pool, rows)
        k_out, v_out = place_pages(from_page, first_seq, second_seq, offsets, arrived, rows, k_out, v_out)
        hidden = jnp.transpose(hidden.reshape(seq_dev, steps, width), (1, 0, 2))
        done = lax.dynamic_slice(finished, (me * seq_dev,), (seq_dev,)) != 0
        live = jnp.stack([jnp.ones_like(done), ~done])
        hidden = jnp.where(live[:, :, None], hidden, jnp.zeros_like(hidden))
        return hidden, k_out, v_out

    in_specs = (rows_spec, full_spec, full_spec, full_spec, full_spec, full_spec, full_spec, pool_spec, pool_spec, table_spec, table_spec, vec_spec, vec_spec, vec_spec, vec_spec)
    return jax.shard_map(device_fn, mesh=mesh, in_specs=in_specs, out_specs=(rows_spec, pool_spec, pool_spec), check_vma=False)
```

time: 1010 us -> 560 us (0.55)
  local copies, waits for them, and re-layouts: 354 us -> 5.03 us
  Pallas kernels: 0 us -> 346 us
  waiting for transfers between devices: 217 us -> 69.7 us
  matrix products: 196 us -> 82 us
  other arithmetic: 103 us -> 8.07 us
  starting transfers between devices: 109 us -> 27.6 us
    pallas_call x0 -> x9, Pallas kernels: none -> 346 us  [the longest x2 190 us: gather_home(): pl.pallas_call(functools.partial(gather_home_kernel, n, q.shape[-1] ** (-...]
    scatter x19 -> x0, local copies, waits for them, and re-layouts: 197 us -> none  [the longest x4 45.9 us: write_new(): k_layer.at[write_rows, offset].set(k_new, mode='drop')]
    dot_general x28 -> x10, matrix products: 196 us -> 82 us  [the longest x2 45.4 us: device_fn(): jnp.dot(inner, w_down[layer], preferred_element_type=jnp.float32)]
    all_gather x4 -> x2, waiting for transfers between devices: 155 us -> 69.6 us  [device_fn(): lax.all_gather(jnp.stack([key, value])[None], 'kv', axis=0, tiled=True)]
    all_to_all x10 -> x3, starting transfers between devices: 108 us -> 27 us  [exchange(): return lax.all_to_all(block, 'kv', 0, 0, tiled=True)]
    gather x31 -> x0, local copies, waits for them, and re-layouts: 78.7 us -> none  [the longest x4 32.9 us: migrate(): outgoing = jnp.stack([k_layer[send_slot], v_layer[send_slot]], axis=1)]
    all_to_all x10 -> x3, waiting for transfers between devices: 61.5 us -> 0.01 us  [exchange(): return lax.all_to_all(block, 'kv', 0, 0, tiled=True)]
    squeeze x4 -> x0, local copies, waits for them, and re-layouts: 46 us -> none  [the longest x2 24.1 us: migrate(): incoming[:, 1]]
  transfers between devices with their start and end apart: 14 -> 5, of which waited for: 6 -> 1; matrix products, arithmetic and copies ran while one was open for 45% -> 16% of each run, Pallas kernels for 0% -> 56%
where the time goes in v1:
time: 560 us; the launch traced here: 553 us
  Pallas kernels  346 us (62%)
  matrix products  82 us (15%)
  waiting for transfers between devices  69.7 us (12%)
  starting transfers between devices  27.6 us (5%)
  between operations  14.4 us (3%)
  other arithmetic  8.07 us (1%)
    pallas_call x2, Pallas kernels, gather_home(): pl.pallas_call(functools.partial(gather_home_kernel, n, q.shape[-1] ** (-...  190 us
    pallas_call x2, Pallas kernels, spread(): pl.pallas_call(functools.partial(spread_kernel, n), out_shape=jax.ShapeDt...  99.5 us
    all_gather x2, waiting for transfers between devices, device_fn(): lax.all_gather(jnp.stack([key, value])[None], 'kv', axis=0, tiled=True)  69.6 us
    dot_general x2, matrix products, device_fn(): jnp.dot(inner, w_down[layer], preferred_element_type=jnp.float32)  45.4 us
    pallas_call x2, Pallas kernels, attend_pages(): pl.pallas_call(functools.partial(attend_kernel, block, pages_seq, seq_dev...  28.4 us
    all_to_all x3, starting transfers between devices, exchange(): return lax.all_to_all(block, 'kv', 0, 0, tiled=True)  27 us
    pallas_call x1, Pallas kernels, place_pages(): pl.pallas_call(functools.partial(place_kernel, depth, lead, n_layers, rou...  16.2 us
  transfers between devices with their start and end apart: 5, of which 1 were waited for; matrix products, arithmetic and copies ran while one was open for 16% of the time, Pallas kernels for 56%

profile of v1, /device:TPU:97, one launch (start us, length us, event | category | flops | bytes accessed | tf_op | source)
XLA Modules:
  0.0 552.8 jit_solution(9895355969399067766)
XLA Ops:
  7.2 0.7 broadcast_compare_fusion
  7.9 0.7 multiply_add_fusion.1
  8.6 0.4 convert_reduce_fusion
  9.0 0.8 copy.28
  9.8 4.6 fusion.61
  14.4 0.6 reshape.97.x_ref.q_ref
  15.0 20.3 %spread_queries.2.q_ref = bf16[2,16,4,32,128]{4,3,2,1,0:T(8,128)(2,1)} custom-call(bf16[4,32,128]{2,1,0:T(8,128)(2,1)} %reshape.97.x_ref.q_ref), custom_call_target="tpu_custom_call" | custom-call | tf_op jit(solution)/shard_map/spread_queries/pallas_call | solution.py:357
  35.3 0.7 broadcast_subtract_fusion.1
  36.0 0.7 select_reduce_fusion.1.slot_ref
  36.8 2.7 pack_pages.1
  39.5 15.3 %all-to-all-start = ((bf16[32,2,2,16,16,128]{5,4,3,2,1,0:T(8,128)(2,1)}), bf16[32,2,2,16,16,128]{5,4,3,2,1,0:T(8,128)(2,1)}, u32[]{:S(2)}, u32[]{:S(2)}) async-start(bf16[32,2,2,16,16,128]{5,4,3,2,1,0:T(8,128)(2,1)} %get-tuple-element.22), calls=%async_computation | async-start | bytes 16777216 | tf_op jit(solution)/shard_map/all_to_all | solution.py:525
  54.8 4.6 fusion.85
  59.4 0.6 copy.32
  60.0 4.6 fusion.88
  64.6 0.6 copy.31
  65.2 0.1 copy.29
  65.3 0.1 sub.81
  65.7 0.7 select_reduce_fusion.code_ref
  66.4 14.2 %attend_pages.2.acc_ref = f32[32,5,32,128]{3,2,1,0:T(8,128)} custom-call(s32[72]{0:T(128)} %select_reduce_fusion.code_ref, bf16[2,16,4,32,128]{4,3,2,1,0:T(8,128)(2,1)} %spread_queries.2.q_ref, bf16[72,2,16,16,128]{4,3,2,1,0:T(8,128)(2,1)} %k_ref.7, bf16[72,2,16,16,128]{4,3,2,1,0:T(8,128)(2,1)} %v_ref.7), custom_call_target="tpu_custom_call" | custom-call | flops 400000000 | bytes 9437184 | tf_op jit(solution)/shard_map/attend_pages/pallas_call | solution.py:256
  80.6 122.6 %gather_home.2 = bf16[4,32,128]{2,1,0:T(8,128)(2,1)} custom-call(f32[32,5,32,128]{3,2,1,0:T(8,128)} %attend_pages.2.acc_ref, bf16[4,32,128]{2,1,0:T(8,128)(2,1)} %reshape.97.x_ref.q_ref, bf16[4,2,16,128]{3,2,1,0:T(8,128)(2,1)} %bitcast.139, bf16[4,2,16,128]{3,2,1,0:T(8,128)(2,1)} %bitcast.137), custom_call_target="tpu_custom_call" | custom-call | tf_op jit(solution)/shard_map/gather_home/pallas_call | solution.py:462
  203.3 5.4 all-to-all-start.1
  208.7 0.2 all-gather.5.cloned.1.call-start
  209.0 0.6 pad_maximum_fusion
  209.7 4.6 fusion.58
  214.3 22.7 %fusion.52 = bf16[8,2048]{1,0:T(8,128)(2,1)S(1)} fusion(bf16[2,8192,2048]{2,1,0:T(8,128)(2,1)} %param.21, bf16[8,2048]{1,0:T(8,128)(2,1)S(1)} %fusion.58, bf16[2,2048,8192]{2,1,0:T(8,128)(2,1)} %param.20), kind=kOutput, calls=%fused_computation.44 | convolution fusion | flops 537509888 | bytes 67207168 | tf_op jit(solution)/shard_map/dot_general | solution.py:550
  237.0 4.6 fusion.79
  241.6 0.6 copy.34
  242.2 4.6 fusion.82
  246.8 0.6 copy.33
  247.4 4.6 fusion.70
  252.0 0.6 reshape.101.x_ref.q_ref
  252.6 79.3 %spread_queries.3.q_ref = bf16[2,16,4,32,128]{4,3,2,1,0:T(8,128)(2,1)} custom-call(bf16[4,32,128]{2,1,0:T(8,128)(2,1)} %reshape.101.x_ref.q_ref), custom_call_target="tpu_custom_call" | custom-call | tf_op jit(solution)/shard_map/spread_queries/pallas_call | solution.py:357
  331.9 14.2 %attend_pages.3.acc_ref = f32[32,5,32,128]{3,2,1,0:T(8,128)} custom-call(s32[72]{0:T(128)} %select_reduce_fusion.code_ref, bf16[2,16,4,32,128]{4,3,2,1,0:T(8,128)(2,1)} %spread_queries.3.q_ref, bf16[72,2,16,16,128]{4,3,2,1,0:T(8,128)(2,1)} %k_ref.7, bf16[72,2,16,16,128]{4,3,2,1,0:T(8,128)(2,1)} %v_ref.7), custom_call_target="tpu_custom_call" | custom-call | flops 400000000 | bytes 9437184 | tf_op jit(solution)/shard_map/attend_pages/pallas_call | solution.py:256
  346.1 67.6 %gather_home.3 = bf16[4,32,128]{2,1,0:T(8,128)(2,1)} custom-call(f32[32,5,32,128]{3,2,1,0:T(8,128)} %attend_pages.3.acc_ref, bf16[4,32,128]{2,1,0:T(8,128)(2,1)} %reshape.101.x_ref.q_ref, bf16[4,2,16,128]{3,2,1,0:T(8,128)(2,1)} %bitcast.143, bf16[4,2,16,128]{3,2,1,0:T(8,128)(2,1)} %bitcast.141), custom_call_target="tpu_custom_call" | custom-call | tf_op jit(solution)/shard_map/gather_home/pallas_call | solution.py:462
  413.7 6.3 %all-to-all-start.2 = ((bf16[32,2,2,16,16,128]{5,4,3,2,1,0:T(8,128)(2,1)}), bf16[32,2,2,16,16,128]{5,4,3,2,1,0:T(8,128)(2,1)}, u32[]{:S(2)}, u32[]{:S(2)}) async-start(bf16[32,2,2,16,16,128]{5,4,3,2,1,0:T(8,128)(2,1)} %get-tuple-element.24), calls=%async_computation.2 | async-start | bytes 16777216 | tf_op jit(solution)/shard_map/all_to_all | solution.py:525
  420.0 0.3 all-gather.7.cloned.1.call-start
  420.3 0.6 pad_maximum_fusion.1
  421.1 4.6 fusion.55
  425.6 22.7 %fusion.49 = bf16[8,2048]{1,0:T(8,128)(2,1)S(1)} fusion(bf16[2,8192,2048]{2,1,0:T(8,128)(2,1)} %param.21, bf16[8,2048]{1,0:T(8,128)(2,1)S(1)} %fusion.55, bf16[2,2048,8192]{2,1,0:T(8,128)(2,1)} %param.20), kind=kOutput, calls=%fused_computation.43 | convolution fusion | flops 537509888 | bytes 67207168 | tf_op jit(solution)/shard_map/dot_general | solution.py:550
  448.5 0.7 subtract_bitcast_fusion.1
  449.2 0.1 select_reduce_fusion.3
  449.3 0.1 select_reduce_fusion.2.from_ref
  449.5 0.5 compare_select_fusion.offset_ref
  450.0 0.5 compare_select_fusion.2.first_ref
  450.5 0.7 bitcast_select_fusion
  451.2 69.6 %all-gather.7.cloned.1.call-done = bf16[64,4,2,16,128]{4,3,2,1,0:T(8,128)(2,1)} async-done(((bf16[2,4,2,16,128]{4,3,2,1,0:T(8,128)(2,1)}), bf16[64,4,2,16,128]{4,3,2,1,0:T(8,128)(2,1)}) %all-gather.7.cloned.1.call-update) | async-done | bytes 2097168 | tf_op jit(solution)/shard_map/all_gather | solution.py:546
  520.7 9.0 %keep_pages.1 = (bf16[72,2,16,16,128]{4,3,2,1,0:T(8,128)(2,1)}, bf16[72,2,16,16,128]{4,3,2,1,0:T(8,128)(2,1)}) custom-call(s32[72]{0:T(128)} %copy-done.7, s32[72]{0:T(128)} %compare_select_fusion.2.first_ref, s32[72]{0:T(128)} %copy-done.6, s32[128]{0:T(128)} %compare_select_fusion.offset_ref, bf16[72,2,16,16,128]{4,3,2,1,0:T(8,128)(2,1)} %k_ref.7, ...), custom_call_target="tpu_custom_call" | custom-call | tf_op jit(solution)/shard_map/keep_pages/pallas_call | solution.py:138
  529.7 16.2 %place_pages.1 = (bf16[72,2,16,16,128]{4,3,2,1,0:T(8,128)(2,1)}, bf16[72,2,16,16,128]{4,3,2,1,0:T(8,128)(2,1)}) custom-call(s32[72]{0:T(128)} %copy-done.7, s32[72]{0:T(128)} %compare_select_fusion.2.first_ref, s32[72]{0:T(128)} %copy-done.6, s32[128]{0:T(128)} %compare_select_fusion.offset_ref, ...), custom_call_target="tpu_custom_call", output_to_operand_aliasing={{0}: (9, {}), {1}: (10, {})} | custom-call | tf_op jit(solution)/shard_map/place_pages/pallas_call | solution.py:188
  (41 shorter events, 0.6 us)
Async XLA Ops:
  39.5 25.8 %copy-start.8 = (s32[128,12]{0,1:T(8,128)S(1)}, s32[128,12]{0,1:T(8,128)}, u32[]{:S(2)}) copy-start(s32[128,12]{0,1:T(8,128)} %param.24) | copy-start | bytes 18436
  39.5 26.0 %copy-start.9 = (s32[128]{0:T(128)S(1)}, s32[128]{0:T(128)}, u32[]{:S(2)}) copy-start(s32[128]{0:T(128)} %param.26) | copy-start | bytes 1540
  39.5 163.8 %all-to-all-start = ((bf16[32,2,2,16,16,128]{5,4,3,2,1,0:T(8,128)(2,1)}), bf16[32,2,2,16,16,128]{5,4,3,2,1,0:T(8,128)(2,1)}, u32[]{:S(2)}, u32[]{:S(2)}) async-start(bf16[32,2,2,16,16,128]{5,4,3,2,1,0:T(8,128)(2,1)} %get-tuple-element.22), calls=%async_computation | async-start | bytes 16777216 | tf_op jit(solution)/shard_map/all_to_all | solution.py:525
  66.4 142.6 %copy-start = (bf16[1,8,16,128]{3,2,1,0:T(8,128)(2,1)S(1)}, bf16[1,8,16,128]{3,2,1,0:T(8,128)(2,1)}, u32[]{:S(2)}) copy-start(bf16[1,8,16,128]{3,2,1,0:T(8,128)(2,1)} %copy.32) | copy-start | bytes 98308
  66.4 142.6 %copy-start.1 = (bf16[1,8,16,128]{3,2,1,0:T(8,128)(2,1)S(1)}, bf16[1,8,16,128]{3,2,1,0:T(8,128)(2,1)}, u32[]{:S(2)}) copy-start(bf16[1,8,16,128]{3,2,1,0:T(8,128)(2,1)} %copy.31) | copy-start | bytes 98308
  203.3 6.4 %copy-start.5 = (bf16[4,32,128]{2,1,0:T(8,128)(2,1)S(1)}, bf16[4,32,128]{2,1,0:T(8,128)(2,1)}, u32[]{:S(2)}) copy-start(bf16[4,32,128]{2,1,0:T(8,128)(2,1)} %gather_home.2) | copy-start | bytes 98308
  203.3 210.4 %all-to-all-start.1 = ((bf16[32,2,2,16,16,128]{5,4,3,2,1,0:T(8,128)(2,1)}), bf16[32,2,2,16,16,128]{5,4,3,2,1,0:T(8,128)(2,1)}, u32[]{:S(2)}, u32[]{:S(2)}) async-start(bf16[32,2,2,16,16,128]{5,4,3,2,1,0:T(8,128)(2,1)} %get-tuple-element.23), calls=%async_computation.1 | async-start | bytes 16777216 | tf_op jit(solution)/shard_map/all_to_all | solution.py:525
  208.7 242.4 %all-gather.5.cloned.1.call-start = ((), (), s32[]{:S(2)}) async-start(), calls=%async_computation.3 | async-start | bytes 2162688 | tf_op jit(solution)/shard_map/all_gather | solution.py:546
  331.9 88.5 %copy-start.2 = (bf16[1,8,16,128]{3,2,1,0:T(8,128)(2,1)S(1)}, bf16[1,8,16,128]{3,2,1,0:T(8,128)(2,1)}, u32[]{:S(2)}) copy-start(bf16[1,8,16,128]{3,2,1,0:T(8,128)(2,1)} %copy.34) | copy-start | bytes 98308
  331.9 88.5 %copy-start.3 = (bf16[1,8,16,128]{3,2,1,0:T(8,128)(2,1)S(1)}, bf16[1,8,16,128]{3,2,1,0:T(8,128)(2,1)}, u32[]{:S(2)}) copy-start(bf16[1,8,16,128]{3,2,1,0:T(8,128)(2,1)} %copy.33) | copy-start | bytes 98308
  413.7 7.3 %copy-start.4 = (bf16[4,32,128]{2,1,0:T(8,128)(2,1)S(1)}, bf16[4,32,128]{2,1,0:T(8,128)(2,1)}, u32[]{:S(2)}) copy-start(bf16[4,32,128]{2,1,0:T(8,128)(2,1)} %gather_home.3) | copy-start | bytes 98308
  413.7 116.0 %all-to-all-start.2 = ((bf16[32,2,2,16,16,128]{5,4,3,2,1,0:T(8,128)(2,1)}), bf16[32,2,2,16,16,128]{5,4,3,2,1,0:T(8,128)(2,1)}, u32[]{:S(2)}, u32[]{:S(2)}) async-start(bf16[32,2,2,16,16,128]{5,4,3,2,1,0:T(8,128)(2,1)} %get-tuple-element.24), calls=%async_computation.2 | async-start | bytes 16777216 | tf_op jit(solution)/shard_map/all_to_all | solution.py:525
  420.0 100.7 %all-gather.7.cloned.1.call-start = ((), (), s32[]{:S(2)}) async-start(), calls=%async_computation.4 | async-start | bytes 2162688 | tf_op jit(solution)/shard_map/all_gather | solution.py:546
  425.6 22.7 %copy-start.10 = (s32[128]{0:T(128)S(1)}, s32[128]{0:T(128)}, u32[]{:S(2)}) copy-start(s32[128]{0:T(128)} %param.27) | copy-start | bytes 1540
  449.3 71.4 %copy-start.6 = (s32[72]{0:T(128)}, s32[72]{0:T(128)S(1)}, u32[]{:S(2)}) copy-start(s32[72]{0:T(128)S(1)} %get-tuple-element.34.second_ref) | copy-start | bytes 868
  449.5 71.3 %copy-start.7 = (s32[72]{0:T(128)}, s32[72]{0:T(128)S(1)}, u32[]{:S(2)}) copy-start(s32[72]{0:T(128)S(1)} %select_reduce_fusion.2.from_ref) | copy-start | bytes 868
Sparse Core Ops, SparseCore 0:
  211.6 99.4 all-gather.4
  423.5 97.1 all-gather.6
